TPU v7x, 128 devices: a whole 4x4x4 slice. The times are simulated.
128 devices in a mesh: dp: 8 (over y, core), list: 16 (over x, z).
Axes of the slice: x: 4, y: 4, z: 4, core: 2. Of those that a mesh axis runs over, the one named last changes fastest.
Arguments:
- embeddings: bfloat16 [65536, 1024], P(('dp', 'list')), may hold values from -6 to 6
- coarse_id: int32 [65536], P(('dp', 'list')), may hold values from 0 to 8191, as said below
- fine_id: int32 [65536], P(('dp', 'list')), may hold values from 0 to 63
- list_home: int32 [8192], replicated, may hold values from 0 to 8191, as said below
- coarse_old: bfloat16 [8192, 1024], P('list'), may hold values from -6 to 6
Outputs:
- residual: bfloat16 [65536, 1024], P(('dp', 'list'))
- coarse_new: float32 [8192, 1024], P('list')
Inputs may be any that keep to these rules, and one draw needn't show every extreme that they name: list_home is a permutation of 0 .. 8191. The device of a row is the one with dp index fine_id // 8 and list index list_home[coarse_id] // 512. Among the rows of one device at most 12 have the same device, and in every draw some device is the device of exactly 12 rows of every device.
All inputs are finite; a program needn't handle non-finite values.
Results may differ from a plain program's by a relative error of at most 0.0055.
Values may be sent and summed in bfloat16 or wider, within the bound.
No kernel may reach another device: no remote copies, remote signals or barrier semaphores. Data moves between devices by JAX's collectives and lax.ppermute only.
A program may use at most 128 MiB of HBM per device.

v0:
```python
import math

import jax
import jax.numpy as jnp
from jax import lax
from jax.sharding import PartitionSpec as P

FINE = 64


def cut_along(shard, dim, size):
    lengths = shard.shape
    parts = shard.reshape(*lengths[:dim], size, lengths[dim] // size, *lengths[dim + 1 :])
    return jnp.moveaxis(parts, dim, 0)


def sum_at_owner(shard, axis, dim):
    size = lax.axis_size(axis)
    parts = lax.all_to_all(cut_along(shard, dim, size), axis, 0, 0, tiled=True)
    return jnp.sum(parts.astype(jnp.float32), axis=0)


def side_by_side(arrays, axis, dim, along):
    columns = [a.reshape(*a.shape[:along], -1) for a in arrays]
    both = jnp.concatenate(columns, axis=along)
    whole, at, done = (sum_at_owner(both, axis, dim), 0, [])
    for a, column in zip(arrays, columns):
        slab = whole[..., at : at + column.shape[along]]
        done.append(slab.reshape(*slab.shape[:along], *a.shape[along:]))
        at += column.shape[along]
    return tuple(done)


def from_everyone(shard, axis):
    copies = jnp.broadcast_to(shard, (lax.axis_size(axis), *shard.shape))
    return lax.all_to_all(copies, axis, split_axis=0, concat_axis=0, tiled=True)


def laid_out(parts, dim):
    lengths = list(parts.shape[1:])
    lengths[dim] *= parts.shape[0]
    return jnp.moveaxis(parts, 0, dim).reshape(lengths)


def collect(shard, axis, dim):
    parts = from_everyone(shard, axis)
    return laid_out(parts, dim)


def on_device(embeddings, coarse_id, fine_id, list_home, coarse_old):
    dp_count = lax.axis_size("dp")
    owners = lax.axis_size("list")
    peers = dp_count * owners
    row_count, width = embeddings.shape
    lists_here = coarse_old.shape[0]
    fine_here = FINE // dp_count
    capacity = 3 * (row_count // peers)
    position = list_home[coarse_id]
    target = fine_id // fine_here * owners + position // lists_here
    marks = (target[:, None] == jnp.arange(peers, dtype=jnp.int32)[None, :]).astype(jnp.int32)
    earlier = jnp.cumsum(marks, axis=0) - marks
    arrival = jnp.sum(earlier * marks, axis=1)
    placed = target * capacity + arrival
    anchor = (
        jnp.full((peers * capacity,), row_count, jnp.int32)
        .at[placed]
        .set(jnp.arange(row_count, dtype=jnp.int32))
    )
    empty_key = lists_here * fine_here
    local_key = position % lists_here * fine_here + fine_id % fine_here
    padded = jnp.concatenate([embeddings, jnp.zeros((1, width), embeddings.dtype)], axis=0)
    keys_padded = jnp.concatenate([local_key, jnp.full((1,), empty_key, jnp.int32)])
    outgoing = padded[anchor].reshape(peers, capacity, width)
    outgoing_keys = keys_padded[anchor].reshape(peers, capacity)
    incoming, incoming_keys = (
        lax.all_to_all(outgoing, ("dp", "list"), split_axis=0, concat_axis=0, tiled=True),
        lax.all_to_all(outgoing_keys, ("dp", "list"), split_axis=0, concat_axis=0, tiled=True),
    )
    total_rows = peers * capacity
    arrived = incoming.reshape(total_rows, width)
    arrived_keys = incoming_keys.reshape(total_rows)
    arrived_slot = arrived_keys // fine_here
    block_rows = math.gcd(total_rows, 1024)
    blocks = total_rows // block_rows
    columns = jnp.arange(lists_here, dtype=jnp.int32)

    def accumulate(carry, item):
        sums_acc, counts_acc = carry
        block_data, block_slot = item
        chosen = block_slot[:, None] == columns[None, :]
        sums_acc = sums_acc + lax.dot_general(
            chosen.astype(jnp.bfloat16),
            block_data,
            (((0,), (0,)), ((), ())),
            preferred_element_type=jnp.float32,
        )
        counts_acc = counts_acc + jnp.sum(chosen.astype(jnp.float32), axis=0)
        return ((sums_acc, counts_acc), None)

    start_state = (
        jnp.zeros((lists_here, width), jnp.float32),
        jnp.zeros((lists_here,), jnp.float32),
    )
    (list_sums, list_counts), _ = lax.scan(
        accumulate,
        start_state,
        (arrived.reshape(blocks, block_rows, width), arrived_slot.reshape(blocks, block_rows)),
    )
    lists_share = lists_here // dp_count
    share_sums, share_counts = side_by_side(
        (list_sums.astype(jnp.bfloat16), list_counts.astype(jnp.bfloat16)), "dp", 0, 1
    )
    share_old = lax.dynamic_slice_in_dim(
        coarse_old, lax.axis_index("dp") * lists_share, lists_share, 0
    )
    share_new = (share_old.astype(jnp.float32) + share_sums) / (1.0 + share_counts)[:, None]
    coarse_new = collect(share_new.astype(jnp.bfloat16), "dp", 0).astype(share_new.dtype)
    coarse_padded = jnp.concatenate([coarse_new, jnp.zeros((1, width), jnp.float32)], axis=0)
    centroid_rows = coarse_padded[arrived_slot]
    centered = arrived.astype(jnp.float32) - centroid_rows
    fine_sums = jax.ops.segment_sum(centered, arrived_keys, num_segments=empty_key + 1)
    fine_counts = jax.ops.segment_sum(
        jnp.ones((total_rows,), jnp.float32), arrived_keys, num_segments=empty_key + 1
    )
    fine_means = fine_sums / (1.0 + fine_counts)[:, None]
    fine_part = fine_means[arrived_keys]
    finished = (centered - fine_part).astype(jnp.bfloat16).reshape(peers, capacity, width)
    returned = lax.all_to_all(finished, ("dp", "list"), split_axis=0, concat_axis=0, tiled=True)
    residual = returned.reshape(total_rows, width)[placed]
    return (residual, coarse_new)


def solution(mesh):
    return jax.shard_map(
        on_device,
        mesh=mesh,
        in_specs=(
            P(("dp", "list"), None),
            P(("dp", "list")),
            P(("dp", "list")),
            P(),
            P("list", None),
        ),
        out_specs=(P(("dp", "list"), None), P("list", None)),
        check_vma=False,
    )
```

profile of v0, /device:TPU:0, one launch (start us, length us, event | category | flops | bytes accessed | tf_op | source)
XLA Modules:
  0.0 309.0 jit_solution(11622079736338455913)
XLA Ops:
  0.6 0.0 copy-start
  0.6 0.7 compare_select_fusion.7
  1.3 0.0 copy-done
  1.4 3.1 %gather_fusion = s32[512]{0:T(512)S(1)} fusion(s32[8192]{0:T(1024)S(1)} %copy-done, s32[1024]{0:T(1024)S(1)} %pad_clamp_fusion.4), kind=kCustom, calls=%fused_computation | custom fusion | bytes 6144 | tf_op jit(solution)/shard_map/gather | solution.py:58
  4.5 0.7 fusion.28
  5.2 0.1 copy.14
  5.3 0.2 fusion.15
  5.7 0.2 fusion.14
  5.9 2.5 scatter_custom_fusion
  8.4 0.0 copy-start.3
  8.4 5.9 %gather_fusion.2 = s32[1536]{0:T(1024)S(1)} fusion(s32[513]{0:T(1024)S(1)} %pad_add_fusion, s32[2048]{0:T(1024)S(1)} %pad_clamp_fusion.2), kind=kCustom, calls=%fused_computation.2 | custom fusion | bytes 18432 | tf_op jit(solution)/shard_map/gather | solution.py:74
  14.3 0.7 all_to_all.19
  15.0 11.2 %all-to-all-start.1 = ((s32[128,1,12]{2,1,0:T(1,128)}), s32[128,1,12]{2,1,0:T(1,128)S(1)}, u32[]{:S(2)}, u32[]{:S(2)}) async-start(s32[128,1,12]{2,1,0:T(1,128)} %bitcast.4), calls=%async_computation.1 | async-start | bytes 131072 | tf_op jit(solution)/shard_map/all_to_all | solution.py:77
  26.2 0.0 copy-done.3
  26.2 0.1 concatenate.17
  26.3 5.9 %gather_fusion.1 = bf16[1536,1024]{1,0:T(8,128)(2,1)} fusion(bf16[513,1024]{1,0:T(8,128)(2,1)S(1)} %concatenate.17, s32[2048]{0:T(1024)S(1)} %pad_clamp_fusion.2), kind=kCustom, calls=%fused_computation.1 | custom fusion | bytes 6297600 | tf_op jit(solution)/shard_map/gather | solution.py:73
  32.1 6.1 %reshape.162 = bf16[128,12,1024]{2,1,0:T(8,128)(2,1)} reshape(bf16[1536,1024]{1,0:T(8,128)(2,1)} %gather_fusion.1) | data formatting | bytes 6291456 | tf_op jit(solution)/shard_map/reshape | solution.py:73
  38.2 0.0 all-to-all-done.1
  38.2 10.3 %all-to-all-start = ((bf16[128,12,1024]{2,1,0:T(8,128)(2,1)}), bf16[128,12,1024]{2,1,0:T(8,128)(2,1)}, u32[]{:S(2)}, u32[]{:S(2)}) async-start(bf16[128,12,1024]{2,1,0:T(8,128)(2,1)} %reshape.162), calls=%async_computation | async-start | bytes 8388608 | tf_op jit(solution)/shard_map/all_to_all | solution.py:76
  48.5 0.5 broadcast.227
  49.1 0.8 reduce.13
  49.9 0.1 reshape.163
  50.0 50.0 %all-to-all-done = bf16[128,12,1024]{2,1,0:T(8,128)(2,1)} async-done(((bf16[128,12,1024]{2,1,0:T(8,128)(2,1)}), bf16[128,12,1024]{2,1,0:T(8,128)(2,1)}, u32[]{:S(2)}, u32[]{:S(2)}) %all-to-all-start) | async-done | bytes 3145760 | tf_op jit(solution)/shard_map/all_to_all | solution.py:76
  100.0 6.2 %reshape_reshape.3 = bf16[3,512,1024]{2,1,0:T(8,128)(2,1)} reshape(bf16[128,12,1024]{2,1,0:T(8,128)(2,1)} %all-to-all-done) | data formatting | bytes 6291456 | tf_op jit(solution)/shard_map/reshape;reshape | solution.py:107
  106.1 8.1 %while.13 = (s32[]{:T(128)}, f32[512,1024]{1,0:T(8,128)S(1)}, f32[512]{0:T(512)S(1)}, s32[3,512]{1,0:T(4,128)S(1)}, bf16[3,512,1024]{2,1,0:T(8,128)(2,1)}, /*index=5*/s32[]{:T(128)}, s32[]{:T(128)}) while((s32[]{:T(128)}, f32[512,1024]{1,0:T(8,128)S(1)}, f32[512]{0:T(512)S(1)}, s32[3,512]{1,0:T(4,128)S(1)}, ...), condition=%wide.region_6.7_spmd.clone, body=%wide.region_4.6_spmd.clone.sunk | while | flops 538968576 | bytes 5259868 | solution.py:104
  106.2 2.5 select_add_fusion.4
  108.6 0.2 fusion.36
  108.9 2.5 select_add_fusion.4
  111.3 0.2 fusion.36
  111.6 2.5 select_add_fusion.4
  114.0 0.2 fusion.36
  114.2 0.2 convert_element_type.49
  114.4 0.3 concatenate.23
  114.7 1.1 pad_maximum_fusion
  115.8 3.6 %all-to-all-start.2 = ((bf16[8,64,1025]{2,1,0:T(8,128)(2,1)}), bf16[8,64,1025]{2,1,0:T(8,128)(2,1)S(1)}, u32[]{:S(2)}, u32[]{:S(2)}) async-start(bf16[8,64,1025]{2,1,0:T(8,128)(2,1)} %pad_maximum_fusion), calls=%async_computation.2 | async-start | bytes 2359296 | tf_op jit(solution)/shard_map/all_to_all | solution.py:19
  119.4 17.3 %all-to-all-done.2 = bf16[8,64,1025]{2,1,0:T(8,128)(2,1)S(1)} async-done(((bf16[8,64,1025]{2,1,0:T(8,128)(2,1)}), bf16[8,64,1025]{2,1,0:T(8,128)(2,1)S(1)}, u32[]{:S(2)}, u32[]{:S(2)}) %all-to-all-start.2) | async-done | bytes 1049632 | tf_op jit(solution)/shard_map/all_to_all | solution.py:19
  136.6 0.2 convert_reduce_fusion
  136.8 0.1 fusion.18
  136.9 1.0 fusion.12
  137.9 1.1 broadcast_in_dim.48
  139.0 3.6 %all-to-all-start.3 = ((bf16[8,64,1024]{2,1,0:T(8,128)(2,1)}), bf16[8,64,1024]{2,1,0:T(8,128)(2,1)S(1)}, u32[]{:S(2)}, u32[]{:S(2)}) async-start(bf16[8,64,1024]{2,1,0:T(8,128)(2,1)} %broadcast_in_dim.48), calls=%async_computation.3 | async-start | bytes 2097152 | tf_op jit(solution)/shard_map/all_to_all | solution.py:36
  142.6 0.1 reshape.164
  142.7 0.1 reshape.226
  142.8 9.4 %scatter_custom_fusion.2 = f32[4097]{0:T(1024)S(1)} fusion(s32[1536]{0:T(1024)S(1)} %reshape.226, f32[1536]{0:T(1024)S(1)} %broadcast.149, f32[]{:T(128)} %constant.110.clone.1), kind=kCustom, calls=%fused_computation.53 | custom fusion | flops 1536 | bytes 16392 | tf_op jit(solution)/shard_map/scatter-add | solution.py:122
  152.2 0.1 fusion.23
  152.3 6.5 %reshape.167 = f32[1536,1024]{1,0:T(8,128)} reshape(bf16[128,12,1024]{2,1,0:T(8,128)(2,1)} %all-to-all-done) | data formatting | bytes 9437184 | tf_op jit(solution)/shard_map/convert_element_type | solution.py:120
  158.8 0.0 all-to-all-done.3
  158.8 0.3 bitcast_convert_fusion
  159.2 0.0 copy-start.2
  159.2 1.3 copy-done.2
  160.5 0.2 concatenate.22
  160.7 5.8 %gather_fusion.3 = f32[1536,1024]{1,0:T(8,128)} fusion(f32[513,1024]{1,0:T(8,128)S(1)} %concatenate.22, s32[2048]{0:T(1024)S(1)} %pad_clamp_fusion.1), kind=kCustom, calls=%fused_computation.3 | custom fusion | bytes 12589056 | tf_op jit(solution)/shard_map/gather | solution.py:119
  166.6 7.8 %gather.26 = f32[128,12,1024]{2,1,0:T(8,128)} reshape(f32[1536,1024]{1,0:T(8,128)} %gather_fusion.3) | data formatting | bytes 12582912 | tf_op jit(solution)/shard_map/gather | solution.py:119
  174.3 21.9 %scatter_custom_fusion.1 = f32[4097,1024]{1,0:T(8,128)} fusion(s32[1536]{0:T(1024)S(1)} %reshape.226, f32[]{:T(128)} %constant.107.clone.1, f32[1536,1024]{1,0:T(8,128)} %reshape.167, f32[1536,1024]{1,0:T(8,128)} %gather_fusion.3), kind=kCustom, calls=%fused_computation.21 | custom fusion | flops 3145728 | bytes 29364228 | tf_op jit(solution)/shard_map/scatter-add | solution.py:121
  196.2 12.9 %broadcast_divide_fusion = f32[4097,1024]{1,0:T(8,128)} fusion(f32[4097,1024]{1,0:T(8,128)} %scatter_custom_fusion.1, f32[4097]{0:T(1024)S(1)} %scatter_custom_fusion.2), kind=kLoop, calls=%fused_computation.20 | loop fusion | flops 4195328 | bytes 33579012 | tf_op jit(solution)/shard_map/div | solution.py:125
  209.1 13.6 %gather_fusion.4 = f32[1536,1024]{1,0:T(8,128)} fusion(f32[4097,1024]{1,0:T(8,128)} %broadcast_divide_fusion, s32[2048]{0:T(1024)S(1)} %pad_clamp_fusion), kind=kCustom, calls=%fused_computation.4 | custom fusion | bytes 12589056 | tf_op jit(solution)/shard_map/gather | solution.py:126
  222.7 7.8 %gather.28 = f32[128,12,1024]{2,1,0:T(8,128)} reshape(f32[1536,1024]{1,0:T(8,128)} %gather_fusion.4) | data formatting | bytes 12582912 | tf_op jit(solution)/shard_map/gather | solution.py:126
  230.5 11.7 %subtract_convert_fusion = bf16[128,12,1024]{2,1,0:T(8,128)(2,1)} fusion(f32[128,12,1024]{2,1,0:T(8,128)} %gather.28, f32[128,12,1024]{2,1,0:T(8,128)} %gather.26, bf16[128,12,1024]{2,1,0:T(8,128)(2,1)} %all-to-all-done), kind=kLoop, calls=%fused_computation.23 | loop fusion | flops 6291456 | bytes 18874368 | tf_op jit(solution)/shard_map/convert_element_type | solution.py:127
  242.2 7.8 %all-to-all-start.4 = ((bf16[128,12,1024]{2,1,0:T(8,128)(2,1)}), bf16[128,12,1024]{2,1,0:T(8,128)(2,1)}, u32[]{:S(2)}, u32[]{:S(2)}) async-start(bf16[128,12,1024]{2,1,0:T(8,128)(2,1)} %subtract_convert_fusion), calls=%async_computation.4 | async-start | bytes 8388608 | tf_op jit(solution)/shard_map/all_to_all | solution.py:128
  250.0 51.4 %all-to-all-done.4 = bf16[128,12,1024]{2,1,0:T(8,128)(2,1)} async-done(((bf16[128,12,1024]{2,1,0:T(8,128)(2,1)}), bf16[128,12,1024]{2,1,0:T(8,128)(2,1)}, u32[]{:S(2)}, u32[]{:S(2)}) %all-to-all-start.4) | async-done | bytes 3145760 | tf_op jit(solution)/shard_map/all_to_all | solution.py:128
  301.5 0.0 copy-start.1
  301.5 4.7 %reshape.165 = bf16[1536,1024]{1,0:T(8,128)(2,1)S(1)} reshape(bf16[128,12,1024]{2,1,0:T(8,128)(2,1)} %all-to-all-done.4) | data formatting | bytes 6291456 | tf_op jit(solution)/shard_map/reshape | solution.py:129
  306.2 2.8 gather_fusion.5
  309.0 0.0 copy-done.1
  (26 shorter events, 0.2 us)
Async XLA Ops:
  0.6 0.8 copy-start
  8.4 17.8 %copy-start.3 = (bf16[512,1024]{1,0:T(8,128)(2,1)S(1)}, bf16[512,1024]{1,0:T(8,128)(2,1)}, u32[]{:S(2)}) copy-start(bf16[512,1024]{1,0:T(8,128)(2,1)} %param.7) | copy-start | bytes 3145732
  15.0 23.2 %all-to-all-start.1 = ((s32[128,1,12]{2,1,0:T(1,128)}), s32[128,1,12]{2,1,0:T(1,128)S(1)}, u32[]{:S(2)}, u32[]{:S(2)}) async-start(s32[128,1,12]{2,1,0:T(1,128)} %bitcast.4), calls=%async_computation.1 | async-start | bytes 131072 | tf_op jit(solution)/shard_map/all_to_all | solution.py:77
  38.2 61.8 %all-to-all-start = ((bf16[128,12,1024]{2,1,0:T(8,128)(2,1)}), bf16[128,12,1024]{2,1,0:T(8,128)(2,1)}, u32[]{:S(2)}, u32[]{:S(2)}) async-start(bf16[128,12,1024]{2,1,0:T(8,128)(2,1)} %reshape.162), calls=%async_computation | async-start | bytes 8388608 | tf_op jit(solution)/shard_map/all_to_all | solution.py:76
  115.8 20.8 %all-to-all-start.2 = ((bf16[8,64,1025]{2,1,0:T(8,128)(2,1)}), bf16[8,64,1025]{2,1,0:T(8,128)(2,1)S(1)}, u32[]{:S(2)}, u32[]{:S(2)}) async-start(bf16[8,64,1025]{2,1,0:T(8,128)(2,1)} %pad_maximum_fusion), calls=%async_computation.2 | async-start | bytes 2359296 | tf_op jit(solution)/shard_map/all_to_all | solution.py:19
  139.0 19.8 %all-to-all-start.3 = ((bf16[8,64,1024]{2,1,0:T(8,128)(2,1)}), bf16[8,64,1024]{2,1,0:T(8,128)(2,1)S(1)}, u32[]{:S(2)}, u32[]{:S(2)}) async-start(bf16[8,64,1024]{2,1,0:T(8,128)(2,1)} %broadcast_in_dim.48), calls=%async_computation.3 | async-start | bytes 2097152 | tf_op jit(solution)/shard_map/all_to_all | solution.py:36
  159.2 1.3 copy-start.2
  242.2 59.2 %all-to-all-start.4 = ((bf16[128,12,1024]{2,1,0:T(8,128)(2,1)}), bf16[128,12,1024]{2,1,0:T(8,128)(2,1)}, u32[]{:S(2)}, u32[]{:S(2)}) async-start(bf16[128,12,1024]{2,1,0:T(8,128)(2,1)} %subtract_convert_fusion), calls=%async_computation.4 | async-start | bytes 8388608 | tf_op jit(solution)/shard_map/all_to_all | solution.py:128
  301.5 7.5 %copy-start.1 = (s32[8192]{0:T(1024)S(1)}, s32[8192]{0:T(1024)}, u32[]{:S(2)}) copy-start(s32[8192]{0:T(1024)} %param.10) | copy-start | bytes 98308
where the time goes:
time: 311 us; the launch traced here: 309 us
  waiting for transfers between devices  119 us (38%)
  local copies, waits for them, and re-layouts  83.3 us (27%)
  other arithmetic  62.2 us (20%)
  starting transfers between devices  36.4 us (12%)
  matrix products  7.38 us (2%)
    all_to_all x1, waiting for transfers between devices, on_device(): lax.all_to_all(finished, ('dp', 'list'), split_axis=0, concat_axis=0, til...  51.4 us
    all_to_all x1, waiting for transfers between devices, on_device(): lax.all_to_all(outgoing, ('dp', 'list'), split_axis=0, concat_axis=0, til...  50 us
    scatter-add x1, other arithmetic, on_device(): jax.ops.segment_sum(centered, arrived_keys, num_segments=empty_key + 1)  21.9 us
    gather x2, local copies, waits for them, and re-layouts, on_device(): fine_part = fine_means[arrived_keys]  21.4 us
    all_to_all x1, waiting for transfers between devices, sum_at_owner(): parts = lax.all_to_all(cut_along(shard, dim, size), axis, 0, 0, tiled=True)  17.3 us
    gather x2, local copies, waits for them, and re-layouts, on_device(): centroid_rows = coarse_padded[arrived_slot]  13.6 us
    div x1, other arithmetic, on_device(): fine_means = fine_sums / (1.0 + fine_counts)[:, None]  12.9 us
    convert_element_type x1, other arithmetic, on_device(): (centered - fine_part).astype(jnp.bfloat16).reshape(peers, capacity, width)  11.7 us
  transfers between devices with their start and end apart: 5, of which 3 were waited for; matrix products, arithmetic and copies ran while one was open for 10% of the time, Pallas kernels for 0%

commit v1 on v0

v1 whole, which is shorter than its diff:
```python
import math

import jax
import jax.numpy as jnp
from jax import lax
from jax.experimental import pallas as pl
from jax.experimental.pallas import tpu as pltpu
from jax.sharding import PartitionSpec as P

FINE = 64
LANES = 128
KEY_ROWS = 8
VMEM_LIMIT = 62 * 1024 * 1024
WHOLE = pl.BlockSpec(memory_space=pltpu.VMEM)
SCALAR = pl.BlockSpec(memory_space=pltpu.SMEM)


def iota(shape, dim):
    return lax.broadcasted_iota(jnp.int32, shape, dim)


def ones_where(mask):
    return jnp.where(mask, 1.0, 0.0).astype(jnp.bfloat16)


def product(a, b, dims=((1,), (0,))):
    return lax.dot_general(a, b, (dims, ((), ())), preferred_element_type=jnp.float32)


def one_row(ref):
    return jnp.concatenate([ref[q : q + 1, :] for q in range(ref.shape[0])], axis=1)


def pack_kernel(cap, owners, slices, lists_here, me_ref, coarse_ref, fine_ref, home_ref, rows_ref, out_ref, placed_ref, keys_ref):
    rows = rows_ref.shape[0]
    block = cap + KEY_ROWS
    coarse, fine = one_row(coarse_ref), one_row(fine_ref)
    table_rows = home_ref.shape[0]
    home = home_ref[...]
    column = ones_where(iota((LANES, rows), 0) == (coarse & (LANES - 1)))
    high = product((home >> 7).astype(jnp.float32).astype(jnp.bfloat16), column)
    low = product((home & 127).astype(jnp.float32).astype(jnp.bfloat16), column)
    in_row = iota((table_rows, rows), 0) == (coarse >> 7)
    position = jnp.sum(jnp.where(in_row, high * 128.0 + low, 0.0), axis=0, keepdims=True).astype(jnp.int32)
    owner = position // lists_here
    slot = position - owner * lists_here
    key = slot * FINE + fine
    mine = iota((owners, rows), 0) == owner
    before = product(ones_where(mine), ones_where(iota((rows, rows), 0) < iota((rows, rows), 1)))
    rank = jnp.sum(jnp.where(mine, before, 0.0), axis=0, keepdims=True).astype(jnp.int32)
    fits = rank < cap
    over = jnp.max(jnp.where(fits, 0.0, 1.0))
    placed_ref[...] = jnp.where(fits, owner * cap + rank, -1)
    lane = (me_ref[0] * cap + rank) & (LANES - 1)
    spread = ones_where(iota((LANES, rows), 0) == jnp.where(fits, lane, -1))
    key_high = jnp.where(mine, ((key >> 8) + 1).astype(jnp.float32), 0.0).astype(jnp.bfloat16)
    key_low = jnp.where(mine, (key & 255).astype(jnp.float32), 0.0).astype(jnp.bfloat16)
    lanes_high = product(key_high, spread, ((1,), (1,)))
    lanes_low = product(key_low, spread, ((1,), (1,)))
    line = iota((KEY_ROWS, LANES), 0)
    keys_ref[...] = jnp.zeros_like(keys_ref)
    for o in range(owners):
        tile = jnp.where(line == 0, lanes_high[o : o + 1, :], jnp.where(line == 1, lanes_low[o : o + 1, :], 0.0))
        keys_ref[o * block + cap : (o + 1) * block, :] = jnp.where(line == 2, over, tile)
    where_to = jnp.where(fits, owner * block + rank, -1)
    place = ones_where(iota((owners * block, rows), 0) == where_to)
    for pair in range(slices // 2):
        both = product(place, rows_ref[:, pair * 2 * LANES : (pair + 1) * 2 * LANES])
        for half in range(2):
            piece = both[:, half * LANES : (half + 1) * LANES] + keys_ref[...]
            out_ref[2 * pair + half, :, :] = piece.astype(jnp.bfloat16)


def lists_kernel(cap, sources, lists_here, got_ref, old_ref, aug_ref, key_ref, split_ref, new_ref, over_ref, tile_ref, raw_ref, sums_ref):
    lane_rows = sources * cap // LANES
    for s in range(0, sources, 16):
        tile_ref[s * KEY_ROWS : (s + 16) * KEY_ROWS, :] = (
            got_ref[s : s + 16, cap : cap + KEY_ROWS, :].astype(jnp.float32).reshape(16 * KEY_ROWS, LANES)
        )
    high = tile_ref[pl.ds(0, sources, stride=KEY_ROWS), :]
    low = tile_ref[pl.ds(1, sources, stride=KEY_ROWS), :]
    over_ref[0, 0] = jnp.max(tile_ref[pl.ds(2, sources, stride=KEY_ROWS), :])
    raw_ref[...] = jnp.where(high > 0.0, (high - 1.0) * 256.0 + low, -1.0).astype(jnp.int32)
    period = LANES // math.gcd(cap, LANES)
    lines = period * cap // LANES
    groups = sources // period
    lane = iota((groups, LANES), 1)
    for r in range(lines):
        first, last = r * LANES // cap, (r * LANES + LANES - 1) // cap
        value = raw_ref[pl.ds(first, groups, stride=period), :]
        for a in range(first + 1, last + 1):
            value = jnp.where(lane >= a * cap - r * LANES, raw_ref[pl.ds(a, groups, stride=period), :], value)
        key_ref[pl.ds(r, groups, stride=lines), :] = value

    per = 2 * period
    chunk = period * cap

    def copy_rows(g, carry):
        base = pl.multiple_of(g * period, period)
        wide = got_ref[pl.ds(base, period), 0:cap, :].astype(jnp.float32).reshape(chunk, LANES)
        aug_ref[pl.ds(pl.multiple_of(g * chunk, LANES), chunk), 0:LANES] = wide.astype(jnp.bfloat16)
        aug_ref[pl.ds(pl.multiple_of(g * chunk, LANES), chunk), LANES : 2 * LANES] = jnp.ones((chunk, LANES), jnp.bfloat16)
        return carry

    lax.fori_loop(0, groups, copy_rows, 0)
    sums_ref[...] = jnp.zeros_like(sums_ref)
    step = 8
    lists = iota((lists_here, LANES), 0)

    def add(t, carry):
        base = t * step
        parts = [ones_where(lists == (key_ref[pl.ds(base + q, 1), :] >> 6)) for q in range(step)]
        chosen = jnp.concatenate(parts, axis=1)
        start = pl.multiple_of(base * LANES, step * LANES)
        sums_ref[...] += product(chosen, aug_ref[pl.ds(start, step * LANES), :])
        return carry

    lax.fori_loop(0, lane_rows // step, add, 0)
    new = (old_ref[...].astype(jnp.float32) + sums_ref[:, 0:LANES]) / (1.0 + sums_ref[:, LANES : 2 * LANES])
    rounded = new.astype(jnp.bfloat16)
    for d in range(new_ref.shape[0]):
        new_ref[d] = rounded
    split_ref[:, 0:LANES] = rounded
    split_ref[:, LANES : 2 * LANES] = (new - rounded.astype(jnp.float32)).astype(jnp.bfloat16)


def cells_kernel(cap, sources, lists_here, aug_ref, key_ref, split_ref, out_ref, turned_ref, total_ref):
    lane_rows = sources * cap // LANES
    high = 4
    step = 8
    block = high * LANES

    def rows_of(b, carry):
        start = pl.multiple_of(b * block, block)
        own = key_ref[pl.ds(b * high, high), :]
        square = jnp.concatenate([own, jnp.full((LANES - high, LANES), -2, jnp.int32)], axis=0)
        turned = square.astype(jnp.float32).T.astype(jnp.int32)
        columns = [jnp.broadcast_to(turned[:, q : q + 1], (LANES, LANES)) for q in range(high)]
        for q in range(high):
            turned_ref[q * LANES : (q + 1) * LANES, :] = columns[q]
        def part_sum(base, count):
            left = turned_ref[...]
            parts = [ones_where(left == key_ref[pl.ds(base + q, 1), :]) for q in range(count)]
            at = base * LANES if isinstance(base, int) else pl.multiple_of(base * LANES, LANES)
            return product(jnp.concatenate(parts, axis=1), aug_ref[pl.ds(at, count * LANES), :])

        if lane_rows <= 48:
            total_ref[...] = sum(part_sum(t, step) for t in range(0, lane_rows, step))
        else:
            total_ref[...] = jnp.zeros_like(total_ref)

            def add(t, inner):
                total_ref[...] += part_sum(t * step, step)
                return inner

            lax.fori_loop(0, lane_rows // step, add, 0)
        slots = turned_ref[...] >> 6
        parts = [ones_where(slots == iota((block, LANES), 1) + q * LANES) for q in range(lists_here // LANES)]
        centre = product(jnp.concatenate(parts, axis=1), split_ref[...])
        own_rows = aug_ref[pl.ds(start, block), 0:LANES].astype(jnp.float32)
        mean = (centre[:, 0:LANES] + centre[:, LANES : 2 * LANES] + total_ref[:, 0:LANES]) / (
            1.0 + total_ref[:, LANES : 2 * LANES]
        )
        out_ref[pl.ds(start, block), :] = (own_rows - mean).astype(jnp.bfloat16)
        return carry

    lax.fori_loop(0, lane_rows // high, rows_of, 0)


def unpack_kernel(cap, owners, slices, placed_ref, back_ref, parts_ref, out_ref, new_ref):
    rows = out_ref.shape[0]
    placed = placed_ref[...].astype(jnp.float32)
    lines = [placed[:, q * LANES : (q + 1) * LANES] for q in range(rows // LANES)]
    column = jnp.concatenate([jnp.broadcast_to(line, (LANES, LANES)).T for line in lines], axis=0).astype(jnp.int32)
    parts = [ones_where(column == iota((rows, LANES), 1) + r * LANES) for r in range(owners * cap // LANES)]
    take = jnp.concatenate(parts, axis=1)
    for d in range(0, slices, 2):
        both = jnp.concatenate([back_ref[d], back_ref[d + 1]], axis=1)
        out_ref[:, d * LANES : (d + 2) * LANES] = product(take, both).astype(jnp.bfloat16)
    for d in range(slices):
        new_ref[:, d * LANES : (d + 1) * LANES] = parts_ref[d].astype(jnp.float32)


def call(kernel, outs, scratch, in_specs, out_specs, flops, name):
    return pl.pallas_call(
        kernel,
        out_shape=outs,
        in_specs=in_specs,
        out_specs=out_specs,
        scratch_shapes=scratch,
        compiler_params=pltpu.CompilerParams(vmem_limit_bytes=VMEM_LIMIT),
        cost_estimate=pl.CostEstimate(flops=flops, bytes_accessed=4 << 20, transcendentals=0),
        name=name,
    )


def iterate(cap, me, mine, coarse, fine, home, embeddings, coarse_old):
    slices, owners = lax.axis_size("dp"), lax.axis_size("list")
    peers = slices * owners
    rows, width = embeddings.shape
    lists_here = coarse_old.shape[0]
    block = cap + KEY_ROWS
    total = peers * cap
    shape = jax.ShapeDtypeStruct
    from functools import partial

    packed, placed = call(
        partial(pack_kernel, cap, owners, slices, lists_here),
        (shape((slices, owners * block, LANES), jnp.bfloat16), shape((1, rows), jnp.int32)),
        [pltpu.VMEM((owners * block, LANES), jnp.float32)],
        [SCALAR, WHOLE, WHOLE, WHOLE, WHOLE],
        (WHOLE, WHOLE),
        4 * rows * owners * block * width,
        "pack",
    )(me, coarse, fine, home, embeddings)
    got = lax.all_to_all(packed.reshape(peers, block, LANES), ("dp", "list"), 0, 0, tiled=True)
    old_part = lax.dynamic_slice_in_dim(coarse_old, mine * LANES, LANES, 1)
    aug, keys, split, new_part, over = call(
        partial(lists_kernel, cap, peers, lists_here),
        (
            shape((total, 2 * LANES), jnp.bfloat16),
            shape((total // LANES, LANES), jnp.int32),
            shape((lists_here, 2 * LANES), jnp.bfloat16),
            shape((slices, lists_here, LANES), jnp.bfloat16),
            shape((1, 1), jnp.float32),
        ),
        [
            pltpu.VMEM((peers * KEY_ROWS, LANES), jnp.float32),
            pltpu.VMEM((peers, LANES), jnp.int32),
            pltpu.VMEM((lists_here, 2 * LANES), jnp.float32),
        ],
        [WHOLE, WHOLE],
        (WHOLE, WHOLE, WHOLE, WHOLE, SCALAR),
        4 * total * lists_here * LANES,
        "lists",
    )(got, old_part)
    new_parts = lax.all_to_all(new_part, "dp", 0, 0, tiled=True)
    done = call(
        partial(cells_kernel, cap, peers, lists_here),
        shape((total, LANES), jnp.bfloat16),
        [pltpu.VMEM((4 * LANES, LANES), jnp.int32), pltpu.VMEM((4 * LANES, 2 * LANES), jnp.float32)],
        [WHOLE, WHOLE, WHOLE],
        WHOLE,
        4 * total * total * LANES,
        "cells",
    )(aug, keys, split)
    back = lax.all_to_all(done.reshape(peers, cap, LANES), ("dp", "list"), 0, 0, tiled=True)

    def finish(placed, back, new_parts):
        return call(
            partial(unpack_kernel, cap, owners, slices),
            (shape((rows, width), jnp.bfloat16), shape((lists_here, width), jnp.float32)),
            [],
            [WHOLE, WHOLE, WHOLE],
            (WHOLE, WHOLE),
            2 * rows * owners * cap * width,
            "unpack",
        )(placed, back.reshape(slices, owners * cap, LANES), new_parts)

    return over, finish, (placed, back, new_parts)


def on_device(embeddings, coarse_id, fine_id, list_home, coarse_old):
    mine = lax.axis_index("dp")
    me = (mine * lax.axis_size("list") + lax.axis_index("list")).reshape(1)
    rows = embeddings.shape[0]
    args = (
        me,
        mine,
        coarse_id.reshape(rows // LANES, LANES),
        fine_id.reshape(rows // LANES, LANES),
        list_home.reshape(-1, LANES),
        embeddings,
        coarse_old,
    )
    capacity, bound = 40, 96
    over, finish, parts = iterate(capacity, *args)

    def again(parts, args):
        _, finish_all, parts_all = iterate(bound, *args)
        return finish_all(*parts_all)

    return lax.cond(over[0, 0] > 0.0, again, lambda parts, args: finish(*parts), parts, args)


def solution(mesh):
    return jax.shard_map(
        on_device,
        mesh=mesh,
        in_specs=(
            P(("dp", "list"), None),
            P(("dp", "list")),
            P(("dp", "list")),
            P(),
            P("list", None),
        ),
        out_specs=(P(("dp", "list"), None), P("list", None)),
        check_vma=False,
    )
```

time: 311 us -> 105 us (0.34)
  local copies, waits for them, and re-layouts: 83.3 us -> 3.7 us
  waiting for transfers between devices: 119 us -> 44 us
  other arithmetic: 62.2 us -> 0 us
  Pallas kernels: 0 us -> 34.3 us
  starting transfers between devices: 36.4 us -> 21.3 us
  matrix products: 7.38 us -> 0 us
    all_to_all x5 -> x3, waiting for transfers between devices: 119 us -> 44 us  [the longest x1 22.9 us: iterate(): lax.all_to_all(packed.reshape(peers, block, LANES), ('dp', 'list'), 0, 0,...]
    gather x8 -> x0, local copies, waits for them, and re-layouts: 52.6 us -> none  [the longest x2 21.4 us: on_device(): fine_part = fine_means[arrived_keys]]
    pallas_call x0 -> x4, Pallas kernels: none -> 34.3 us  [the longest x1 20.6 us: iterate(): call(partial(cells_kernel, cap, peers, lists_here), shape((total, LANES),...]
    scatter-add x2 -> x0, other arithmetic: 31.2 us -> none  [the longest x1 21.9 us: on_device(): jax.ops.segment_sum(centered, arrived_keys, num_segments=empty_key + 1)]
    all_to_all x5 -> x3, starting transfers between devices: 36.4 us -> 21.3 us  [the longest x1 11.2 us: iterate(): lax.all_to_all(packed.reshape(peers, block, LANES), ('dp', 'list'), 0, 0,...]
    convert_element_type x5 -> x0, other arithmetic: 13.2 us -> none  [the longest x1 11.7 us: on_device(): (centered - fine_part).astype(jnp.bfloat16).reshape(peers, capacity, width)]
    div x1 -> x0, other arithmetic: 12.9 us -> none  [on_device(): fine_means = fine_sums / (1.0 + fine_counts)[:, None]]
    reshape x5 -> x0, local copies, waits for them, and re-layouts: 11.1 us -> none  [the longest x1 6.07 us: on_device(): outgoing = padded[anchor].reshape(peers, capacity, width)]
  transfers between devices with their start and end apart: 5 -> 3, of which waited for: 3 -> 2; matrix products, arithmetic and copies ran while one was open for 10% -> 1% of each run, Pallas kernels for 0% -> 20%
where the time goes in v1:
time: 105 us
  waiting for transfers between devices  44 us (42%)
  Pallas kernels  34.3 us (33%)
  starting transfers between devices  21.3 us (20%)
  local copies, waits for them, and re-layouts  3.7 us (4%)
  between operations  1.33 us (1%)
    all_to_all x1, waiting for transfers between devices, iterate(): lax.all_to_all(packed.reshape(peers, block, LANES), ('dp', 'list'), 0, 0,...  22.9 us
    all_to_all x1, waiting for transfers between devices, iterate(): lax.all_to_all(done.reshape(peers, cap, LANES), ('dp', 'list'), 0, 0, til...  21.1 us
    pallas_call x1, Pallas kernels, iterate(): call(partial(cells_kernel, cap, peers, lists_here), shape((total, LANES),...  20.6 us
    all_to_all x1, starting transfers between devices, iterate(): lax.all_to_all(packed.reshape(peers, block, LANES), ('dp', 'list'), 0, 0,...  11.2 us
    all_to_all x1, starting transfers between devices, iterate(): lax.all_to_all(done.reshape(peers, cap, LANES), ('dp', 'list'), 0, 0, til...  6.6 us
    pallas_call x1, Pallas kernels, iterate(): call(partial(lists_kernel, cap, peers, lists_here), (shape((total, 2 * LA...  5.71 us
    pallas_call x1, Pallas kernels, finish(): call(partial(unpack_kernel, cap, owners, slices), (shape((rows, width), j...  4.09 us
    pallas_call x1, Pallas kernels, iterate(): call(partial(pack_kernel, cap, owners, slices, lists_here), (shape((slice...  3.84 us
  transfers between devices with their start and end apart: 3, of which 2 were waited for; matrix products, arithmetic and copies ran while one was open for 1% of the time, Pallas kernels for 20%

profile of v1, /device:TPU:0, one launch (start us, length us, event | category | flops | bytes accessed | tf_op | source)
XLA Modules:
  0.0 104.7 jit_solution(4228884329771839796)
XLA Ops:
  0.6 3.8 %pack.3 = (bf16[8,768,128]{2,1,0:T(8,128)(2,1)}, s32[1,512]{1,0:T(1,128)S(1)}) custom-call(s32[1]{0:T(128)} %bitcast.4.me_ref, s32[4,128]{1,0:T(4,128)} %bitcast.19, s32[4,128]{1,0:T(4,128)} %bitcast.21, s32[64,128]{1,0:T(8,128)} %bitcast.17, bf16[512,1024]{1,0:T(8,128)(2,1)} %rows_ref.1), custom_call_target="tpu_custom_call" | custom-call | flops 1610612736 | bytes 4194304 | tf_op jit(solution)/shard_map/pack/pallas_call | solution.py:207
  4.5 11.2 %all-to-all-start.3 = ((bf16[128,48,128]{2,1,0:T(8,128)(2,1)}), bf16[128,48,128]{2,1,0:T(8,128)(2,1)S(1)}, u32[]{:S(2)}, u32[]{:S(2)}) async-start(bf16[128,48,128]{2,1,0:T(8,128)(2,1)} %bitcast.14), calls=%async_computation.3 | async-start | bytes 3145728 | tf_op jit(solution)/shard_map/all_to_all | solution.py:216
  15.7 1.6 %constant_dynamic-slice_fusion.1.old_ref = bf16[512,128]{1,0:T(8,128)(2,1)} fusion(bf16[512,1024]{1,0:T(8,128)(2,1)} %param.11, s32[]{:T(128)S(6)} %select_n.6), kind=kLoop, calls=%fused_computation.1 | loop fusion | bytes 262148 | tf_op jit(solution)/shard_map/dynamic_slice | solution.py:217
  17.2 22.9 %all-to-all-done.3.got_ref = bf16[128,48,128]{2,1,0:T(8,128)(2,1)S(1)} async-done(((bf16[128,48,128]{2,1,0:T(8,128)(2,1)}), bf16[128,48,128]{2,1,0:T(8,128)(2,1)S(1)}, u32[]{:S(2)}, u32[]{:S(2)}) %all-to-all-start.3) | async-done | bytes 1572896 | tf_op jit(solution)/shard_map/all_to_all | solution.py:216
  40.1 0.0 copy-start
  40.1 1.1 %copy-done = bf16[128,48,128]{2,1,0:T(8,128)(2,1)} copy-done((bf16[128,48,128]{2,1,0:T(8,128)(2,1)}, bf16[128,48,128]{2,1,0:T(8,128)(2,1)S(1)}, u32[]{:S(2)}) %copy-start) | copy-done | bytes 1572888
  41.3 5.7 %lists.3 = (bf16[5120,256]{1,0:T(8,128)(2,1)}, s32[40,128]{1,0:T(8,128)}, bf16[512,256]{1,0:T(8,128)(2,1)}, bf16[8,512,128]{2,1,0:T(8,128)(2,1)}, f32[1,1]{1,0:T(1,128)}) custom-call(bf16[128,48,128]{2,1,0:T(8,128)(2,1)} %copy-done, bf16[512,128]{1,0:T(8,128)(2,1)} %constant_dynamic-slice_fusion.1.old_ref), custom_call_target="tpu_custom_call" | custom-call | flops 1342177280 | bytes 4194304 | tf_op jit(solution)/shard_map/lists/pallas_call | solution.py:218
  47.0 3.6 %all-to-all-start.5 = ((bf16[8,512,128]{2,1,0:T(8,128)(2,1)}), bf16[8,512,128]{2,1,0:T(8,128)(2,1)S(1)}, u32[]{:S(2)}, u32[]{:S(2)}) async-start(bf16[8,512,128]{2,1,0:T(8,128)(2,1)} %get-tuple-element.51), calls=%async_computation.5 | async-start | bytes 2097152 | tf_op jit(solution)/shard_map/all_to_all | solution.py:237
  50.6 20.6 %cells.3 = bf16[5120,128]{1,0:T(8,128)(2,1)} custom-call(bf16[5120,256]{1,0:T(8,128)(2,1)} %get-tuple-element.47.aug_ref, s32[40,128]{1,0:T(8,128)} %get-tuple-element.48.key_ref, bf16[512,256]{1,0:T(8,128)(2,1)} %get-tuple-element.49.split_ref), custom_call_target="tpu_custom_call" | custom-call | flops 13421772800 | bytes 4194304 | tf_op jit(solution)/shard_map/cells/pallas_call | solution.py:238
  71.2 0.0 copy-start.3
  71.2 0.0 copy-start.4
  71.2 0.0 copy-start.5
  71.2 0.0 all-to-all-done.5
  71.2 0.0 copy-start.1
  71.2 1.0 copy-done.1
  72.2 6.6 %all-to-all-start.4 = ((bf16[128,40,128]{2,1,0:T(8,128)(2,1)}), bf16[128,40,128]{2,1,0:T(8,128)(2,1)S(1)}, u32[]{:S(2)}, u32[]{:S(2)}) async-start(bf16[128,40,128]{2,1,0:T(8,128)(2,1)} %bitcast.16), calls=%async_computation.4 | async-start | bytes 2621440 | tf_op jit(solution)/shard_map/all_to_all | solution.py:247
  79.5 21.1 %all-to-all-done.4 = bf16[128,40,128]{2,1,0:T(8,128)(2,1)S(1)} async-done(((bf16[128,40,128]{2,1,0:T(8,128)(2,1)}), bf16[128,40,128]{2,1,0:T(8,128)(2,1)S(1)}, u32[]{:S(2)}, u32[]{:S(2)}) %all-to-all-start.4) | async-done | bytes 1310752 | tf_op jit(solution)/shard_map/all_to_all | solution.py:247
  100.6 0.0 copy-done.3
  100.6 0.0 copy-done.4
  100.6 0.0 copy-done.5
  100.6 4.1 %conditional.1 = ((bf16[512,1024]{1,0:T(8,128)(2,1)}, f32[512,1024]{1,0:T(8,128)})) conditional(s32[]{:T(128)} %bitcast.9, (bf16[128,40,128]{2,1,0:T(8,128)(2,1)S(1)}, s32[1,512]{1,0:T(1,128)S(1)}, bf16[8,512,128]{2,1,0:T(8,128)(2,1)}) %tuple.23, (s32[1]{0:T(128)}, s32[4,128]{1,0:T(4,128)S(1)}, s32[4,128]{1,0:T(4,128)S(1)}, s32[64,128]{1,0:T(8,128)S(1)}, ...), branch_computations={%region_0.0_spmd, %region_1.0_spmd} | conditional | flops 85630910464 | bytes 40894616 | solution.py:283
  100.6 4.1 %unpack.2 = (bf16[512,1024]{1,0:T(8,128)(2,1)}, f32[512,1024]{1,0:T(8,128)}) custom-call(s32[1,512]{1,0:T(1,128)S(1)} %get-tuple-element.20.placed_ref, bf16[8,640,128]{2,1,0:T(8,128)(2,1)S(1)} %bitcast.15, bf16[8,512,128]{2,1,0:T(8,128)(2,1)} %get-tuple-element.22.parts_ref), custom_call_target="tpu_custom_call" | custom-call | flops 671088640 | bytes 4194304 | tf_op jit(solution)/shard_map/cond/branch_0_fun/unpack/pallas_call | solution.py:250
Async XLA Ops:
  4.5 35.6 %all-to-all-start.3 = ((bf16[128,48,128]{2,1,0:T(8,128)(2,1)}), bf16[128,48,128]{2,1,0:T(8,128)(2,1)S(1)}, u32[]{:S(2)}, u32[]{:S(2)}) async-start(bf16[128,48,128]{2,1,0:T(8,128)(2,1)} %bitcast.14), calls=%async_computation.3 | async-start | bytes 3145728 | tf_op jit(solution)/shard_map/all_to_all | solution.py:216
  40.1 1.1 %copy-start = (bf16[128,48,128]{2,1,0:T(8,128)(2,1)}, bf16[128,48,128]{2,1,0:T(8,128)(2,1)S(1)}, u32[]{:S(2)}) copy-start(bf16[128,48,128]{2,1,0:T(8,128)(2,1)S(1)} %all-to-all-done.3.got_ref) | copy-start | bytes 4718596
  47.0 24.2 %all-to-all-start.5 = ((bf16[8,512,128]{2,1,0:T(8,128)(2,1)}), bf16[8,512,128]{2,1,0:T(8,128)(2,1)S(1)}, u32[]{:S(2)}, u32[]{:S(2)}) async-start(bf16[8,512,128]{2,1,0:T(8,128)(2,1)} %get-tuple-element.51), calls=%async_computation.5 | async-start | bytes 2097152 | tf_op jit(solution)/shard_map/all_to_all | solution.py:237
  71.2 29.4 %copy-start.3 = (s32[8192]{0:T(1024)S(1)}, s32[8192]{0:T(1024)}, u32[]{:S(2)}) copy-start(s32[8192]{0:T(1024)} %param.10) | copy-start | bytes 98308
  71.2 29.4 %copy-start.4 = (s32[512]{0:T(512)S(1)}, s32[512]{0:T(512)}, u32[]{:S(2)}) copy-start(s32[512]{0:T(512)} %param.8) | copy-start | bytes 6148
  71.2 29.4 %copy-start.5 = (s32[512]{0:T(512)S(1)}, s32[512]{0:T(512)}, u32[]{:S(2)}) copy-start(s32[512]{0:T(512)} %param.9) | copy-start | bytes 6148
  71.2 1.0 copy-start.1
  72.2 28.3 %all-to-all-start.4 = ((bf16[128,40,128]{2,1,0:T(8,128)(2,1)}), bf16[128,40,128]{2,1,0:T(8,128)(2,1)S(1)}, u32[]{:S(2)}, u32[]{:S(2)}) async-start(bf16[128,40,128]{2,1,0:T(8,128)(2,1)} %bitcast.16), calls=%async_computation.4 | async-start | bytes 2621440 | tf_op jit(solution)/shard_map/all_to_all | solution.py:247

commit v2 on v1

v2 whole, which is shorter than its diff:
```python
from functools import partial

import jax
import jax.numpy as jnp
from jax import lax
from jax.experimental import pallas as pl
from jax.experimental.pallas import tpu as pltpu
from jax.sharding import PartitionSpec as P

FINE = 64
LANES = 128
KEY_ROWS = 8
HIGH = 4
MIB = 1024 * 1024
WHOLE = pl.BlockSpec(memory_space=pltpu.VMEM)
SCALAR = pl.BlockSpec(memory_space=pltpu.SMEM)


def iota(shape, dim):
    return lax.broadcasted_iota(jnp.int32, shape, dim)


def ones_where(mask):
    return jnp.where(mask, 1.0, 0.0).astype(jnp.bfloat16)


def product(a, b, dims=((1,), (0,))):
    return lax.dot_general(a, b, (dims, ((), ())), preferred_element_type=jnp.float32)


def one_row(ref):
    return jnp.concatenate([ref[q : q + 1, :] for q in range(ref.shape[0])], axis=1)


def pack_kernel(cap, owners, slices, lists_here, coarse_ref, fine_ref, home_ref, rows_ref, out_ref, placed_ref, keys_ref):
    rows = rows_ref.shape[0]
    block = cap + KEY_ROWS
    peers = owners * slices
    coarse, fine = one_row(coarse_ref), one_row(fine_ref)
    table_rows = home_ref.shape[0]
    home = home_ref[...]
    column = ones_where(iota((LANES, rows), 0) == (coarse & (LANES - 1)))
    high = product((home >> 7).astype(jnp.float32).astype(jnp.bfloat16), column)
    low = product((home & 127).astype(jnp.float32).astype(jnp.bfloat16), column)
    in_row = iota((table_rows, rows), 0) == (coarse >> 7)
    position = jnp.sum(jnp.where(in_row, high * 128.0 + low, 0.0), axis=0, keepdims=True).astype(jnp.int32)
    owner = position // lists_here
    slot = position - owner * lists_here
    key = slot * FINE + fine
    target = ones_where(iota((peers, rows), 0) == owner * slices + fine // (FINE // slices))
    before = product(target, ones_where(iota((rows, rows), 0) < iota((rows, rows), 1)))
    counts = product(target, jnp.ones((rows, LANES), jnp.bfloat16))
    line, other = iota((peers, peers), 0), iota((peers, peers), 1)
    lower = ones_where((other < line) & (other // slices == line // slices))
    base = product(lower, counts.astype(jnp.bfloat16))
    base = jnp.concatenate([base] * (rows // LANES), axis=1)
    picked = jnp.where(target.astype(jnp.float32) > 0.0, before + base, 0.0)
    rank = jnp.sum(picked, axis=0, keepdims=True).astype(jnp.int32)
    fits = rank < cap
    over = jnp.max(jnp.where(fits, 0.0, 1.0))
    placed_ref[...] = jnp.where(fits, owner * cap + rank, -1)
    mine = iota((owners, rows), 0) == owner
    spread = ones_where(iota((LANES, rows), 0) == jnp.where(fits, rank, -1))
    key_high = jnp.where(mine, ((key >> 8) + 1).astype(jnp.float32), 0.0).astype(jnp.bfloat16)
    key_low = jnp.where(mine, (key & 255).astype(jnp.float32), 0.0).astype(jnp.bfloat16)
    lanes_high = product(key_high, spread, ((1,), (1,)))
    lanes_low = product(key_low, spread, ((1,), (1,)))
    line = iota((KEY_ROWS, LANES), 0)
    keys_ref[...] = jnp.zeros_like(keys_ref)
    for o in range(owners):
        tile = jnp.where(line == 0, lanes_high[o : o + 1, :], jnp.where(line == 1, lanes_low[o : o + 1, :], 0.0))
        keys_ref[o * block + cap : (o + 1) * block, :] = jnp.where(line == 2, over, tile)
    where_to = jnp.where(fits, owner * block + rank, -1)
    place = ones_where(iota((owners * block, rows), 0) == where_to)
    for pair in range(slices // 2):
        both = product(place, rows_ref[:, pair * 2 * LANES : (pair + 1) * 2 * LANES])
        for half in range(2):
            piece = both[:, half * LANES : (half + 1) * LANES] + keys_ref[...]
            out_ref[2 * pair + half, :, :] = piece.astype(jnp.bfloat16)


def lists_kernel(cap, sources, lists_here, fine_here, got_ref, old_ref, aug_ref, key_ref, span_ref, split_ref, new_ref, over_ref, tile_ref):
    for s in range(0, sources, 16):
        tile_ref[s * KEY_ROWS : (s + 16) * KEY_ROWS, :] = (
            got_ref[s : s + 16, cap : cap + KEY_ROWS, :].astype(jnp.float32).reshape(16 * KEY_ROWS, LANES)
        )
    high = tile_ref[pl.ds(0, sources, stride=KEY_ROWS), :]
    low = tile_ref[pl.ds(1, sources, stride=KEY_ROWS), :]
    over_ref[0, 0] = jnp.max(tile_ref[pl.ds(2, sources, stride=KEY_ROWS), :])
    raw = jnp.where(high > 0.0, (high - 1.0) * 256.0 + low, -1.0)
    key_ref[...] = raw.T.astype(jnp.int32)

    keys = raw.astype(jnp.int32)
    group = (keys & (FINE - 1)) // fine_here
    least = jnp.min(jnp.where(keys >= 0, group, FINE), axis=0, keepdims=True)
    most = jnp.max(jnp.where(keys >= 0, group, -1), axis=0, keepdims=True)
    blocks = span_ref.shape[0]
    lane = iota((blocks, LANES), 1)
    inside = lane // HIGH == iota((blocks, LANES), 0)
    first = jnp.min(jnp.where(inside, least, FINE), axis=1, keepdims=True)
    last = jnp.max(jnp.where(inside, most, -1), axis=1, keepdims=True)
    meet = (most >= first) & (least <= last)
    start = jnp.min(jnp.where(meet, lane, LANES), axis=1, keepdims=True)
    stop = jnp.max(jnp.where(meet, lane + 1, 0), axis=1, keepdims=True)
    span_ref[...] = jnp.where(lane == 0, start, stop)

    part = 16
    for s in range(0, sources, part):
        wide = got_ref[s : s + part, 0:cap, :].astype(jnp.float32)
        aug_ref[:, s : s + part, 0:LANES] = jnp.transpose(wide, (1, 0, 2)).astype(jnp.bfloat16)
    aug_ref[:, :, LANES : 2 * LANES] = jnp.ones((cap, sources, LANES), jnp.bfloat16)
    step = 8
    lists = iota((lists_here, LANES), 0)

    def part_sum(base):
        parts = [ones_where(lists == (key_ref[base + q : base + q + 1, :] >> 6)) for q in range(step)]
        return product(jnp.concatenate(parts, axis=1), aug_ref[base : base + step].reshape(step * sources, 2 * LANES))

    sums = sum(part_sum(t) for t in range(0, cap, step))
    new = (old_ref[...].astype(jnp.float32) + sums[:, 0:LANES]) / (1.0 + sums[:, LANES : 2 * LANES])
    rounded = new.astype(jnp.bfloat16)
    for d in range(new_ref.shape[0]):
        new_ref[d] = rounded
    split_ref[:, 0:LANES] = rounded
    split_ref[:, LANES : 2 * LANES] = (new - rounded.astype(jnp.float32)).astype(jnp.bfloat16)


def cells_kernel(cap, sources, lists_here, aug_ref, key_ref, span_ref, split_ref, out_ref, total_ref, done_ref):
    step = 16 if cap > 16 else cap
    block = HIGH * sources

    def rows_of(b, carry):
        first, stop = span_ref[b, 0], span_ref[b, 1]
        start = pl.multiple_of(b * block, block)

        @pl.when(first >= stop)
        def _():
            done_ref[pl.ds(start, block), :] = jnp.zeros((block, LANES), jnp.float32)

        @pl.when(first < stop)
        def _():
            own = key_ref[pl.ds(b * HIGH, HIGH), :]
            square = jnp.concatenate([own, jnp.full((LANES - HIGH, LANES), -2, jnp.int32)], axis=0)
            turned = square.astype(jnp.float32).T.astype(jnp.int32)
            left = jnp.concatenate(
                [jnp.broadcast_to(turned[:, q : q + 1], (LANES, LANES)) for q in range(HIGH)], axis=0
            )

            def part_sum(t):
                wanted = first + t * step
                base = jnp.minimum(wanted, cap - step)
                parts = []
                for q in range(step):
                    row = key_ref[pl.ds(base + q, 1), :]
                    parts.append(ones_where(left == jnp.where(base + q >= wanted, row, -3)))
                right = aug_ref[pl.ds(base, step)].reshape(step * sources, 2 * LANES)
                return product(jnp.concatenate(parts, axis=1), right)

            slots = left >> 6
            parts = [ones_where(slots == iota((block, LANES), 1) + q * LANES) for q in range(lists_here // LANES)]
            centre = product(jnp.concatenate(parts, axis=1), split_ref[...])
            centre = centre[:, 0:LANES] + centre[:, LANES : 2 * LANES]
            total = part_sum(0)
            total_ref[:, 0:LANES] = total[:, 0:LANES] + centre
            total_ref[:, LANES : 2 * LANES] = total[:, LANES : 2 * LANES] + 1.0

            def more(t, inner):
                total_ref[...] += part_sum(t)
                return inner

            lax.fori_loop(1, (stop - first + step - 1) // step, more, 0)
            own_rows = aug_ref[pl.ds(b * HIGH, HIGH), :, 0:LANES].astype(jnp.float32).reshape(block, LANES)
            mean = total_ref[:, 0:LANES] / total_ref[:, LANES : 2 * LANES]
            done_ref[pl.ds(start, block), :] = own_rows - mean

        return carry

    lax.fori_loop(0, cap // HIGH, rows_of, 0)
    part = 16
    for s in range(0, sources, part):
        piece = jnp.concatenate(
            [done_ref[k * sources + s : k * sources + s + part, :].reshape(1, part, LANES) for k in range(cap)], axis=0
        )
        out_ref[s : s + part] = jnp.transpose(piece, (1, 0, 2)).astype(jnp.bfloat16)


def unpack_kernel(cap, owners, slices, placed_ref, back_ref, parts_ref, out_ref, new_ref):
    rows = out_ref.shape[0]
    placed = placed_ref[...].astype(jnp.float32)
    lines = [placed[:, q * LANES : (q + 1) * LANES] for q in range(rows // LANES)]
    column = jnp.concatenate([jnp.broadcast_to(line, (LANES, LANES)).T for line in lines], axis=0).astype(jnp.int32)
    parts = [ones_where(column == iota((rows, LANES), 1) + r * LANES) for r in range(owners * cap // LANES)]
    take = jnp.concatenate(parts, axis=1)
    for d in range(0, slices, 2):
        both = jnp.concatenate([back_ref[d], back_ref[d + 1]], axis=1)
        out_ref[:, d * LANES : (d + 2) * LANES] = product(take, both).astype(jnp.bfloat16)
    for d in range(slices):
        new_ref[:, d * LANES : (d + 1) * LANES] = parts_ref[d].astype(jnp.float32)


def call(kernel, outs, scratch, in_specs, out_specs, flops, name, mib):
    return pl.pallas_call(
        kernel,
        out_shape=outs,
        in_specs=in_specs,
        out_specs=out_specs,
        scratch_shapes=scratch,
        compiler_params=pltpu.CompilerParams(vmem_limit_bytes=mib * MIB),
        cost_estimate=pl.CostEstimate(flops=flops, bytes_accessed=4 * MIB, transcendentals=0),
        name=name,
    )


def iterate(cap, mine, coarse, fine, home, embeddings, coarse_old):
    slices, owners = lax.axis_size("dp"), lax.axis_size("list")
    peers = slices * owners
    rows, width = embeddings.shape
    lists_here = coarse_old.shape[0]
    block = cap + KEY_ROWS
    total = peers * cap
    mib = 16 if cap <= 48 else 40
    shape = jax.ShapeDtypeStruct

    packed, placed = call(
        partial(pack_kernel, cap, owners, slices, lists_here),
        (shape((slices, owners * block, LANES), jnp.bfloat16), shape((1, rows), jnp.int32)),
        [pltpu.VMEM((owners * block, LANES), jnp.float32)],
        [WHOLE, WHOLE, WHOLE, WHOLE],
        (WHOLE, WHOLE),
        4 * rows * owners * block * width,
        "pack",
        mib,
    )(coarse, fine, home, embeddings)
    got = lax.all_to_all(packed.reshape(peers, block, LANES), ("dp", "list"), 0, 0, tiled=True)
    old_part = lax.dynamic_slice_in_dim(coarse_old, mine * LANES, LANES, 1)
    aug, keys, span, split, new_part, over = call(
        partial(lists_kernel, cap, peers, lists_here, FINE // slices),
        (
            shape((cap, peers, 2 * LANES), jnp.bfloat16),
            shape((LANES, peers), jnp.int32),
            shape((-(-cap // (8 * HIGH)) * 8, LANES), jnp.int32),
            shape((lists_here, 2 * LANES), jnp.bfloat16),
            shape((slices, lists_here, LANES), jnp.bfloat16),
            shape((1, 1), jnp.float32),
        ),
        [pltpu.VMEM((peers * KEY_ROWS, LANES), jnp.float32)],
        [WHOLE, WHOLE],
        (WHOLE, WHOLE, WHOLE, WHOLE, WHOLE, SCALAR),
        4 * total * lists_here * LANES,
        "lists",
        mib,
    )(got, old_part)
    new_parts = lax.all_to_all(new_part, "dp", 0, 0, tiled=True)
    done = call(
        partial(cells_kernel, cap, peers, lists_here),
        shape((peers, cap, LANES), jnp.bfloat16),
        [pltpu.VMEM((HIGH * LANES, 2 * LANES), jnp.float32), pltpu.VMEM((total, LANES), jnp.float32)],
        [WHOLE, WHOLE, SCALAR, WHOLE],
        WHOLE,
        4 * total * total * LANES,
        "cells",
        mib,
    )(aug, keys, span, split)
    back = lax.all_to_all(done, ("dp", "list"), 0, 0, tiled=True)

    def finish(placed, back, new_parts):
        return call(
            partial(unpack_kernel, cap, owners, slices),
            (shape((rows, width), jnp.bfloat16), shape((lists_here, width), jnp.float32)),
            [],
            [WHOLE, WHOLE, WHOLE],
            (WHOLE, WHOLE),
            2 * rows * owners * cap * width,
            "unpack",
            mib,
        )(placed, back.reshape(slices, owners * cap, LANES), new_parts)

    return over, finish, (placed, back, new_parts)


def on_device(embeddings, coarse_id, fine_id, list_home, coarse_old):
    rows = embeddings.shape[0]
    args = (
        lax.axis_index("dp"),
        coarse_id.reshape(rows // LANES, LANES),
        fine_id.reshape(rows // LANES, LANES),
        list_home.reshape(-1, LANES),
        embeddings,
        coarse_old,
    )
    capacity, bound = 40, 96
    over, finish, parts = iterate(capacity, *args)

    def again(parts, args):
        _, finish_all, parts_all = iterate(bound, *args)
        return finish_all(*parts_all)

    return lax.cond(over[0, 0] > 0.0, again, lambda parts, args: finish(*parts), parts, args)


def solution(mesh):
    return jax.shard_map(
        on_device,
        mesh=mesh,
        in_specs=(
            P(("dp", "list"), None),
            P(("dp", "list")),
            P(("dp", "list")),
            P(),
            P("list", None),
        ),
        out_specs=(P(("dp", "list"), None), P("list", None)),
        check_vma=False,
    )
```

time: 105 us -> 95.9 us (0.913); the launches traced: 105 us -> 94.4 us
  Pallas kernels: 34.3 us -> 20.6 us
  waiting for transfers between devices: 44 us -> 48.2 us
  starting transfers between devices: 21.3 us -> 20 us
    pallas_call x2, Pallas kernels: 26.4 us -> 13.7 us  [the longest x1 10.5 us: iterate(): call(partial(cells_kernel, cap, peers, lists_here), shape((peers, cap, LA...]
    all_to_all x1, waiting for transfers between devices: 0.01 us -> 3.62 us  [iterate(): new_parts = lax.all_to_all(new_part, 'dp', 0, 0, tiled=True)]
    all_to_all x1, starting transfers between devices: 6.6 us -> 5.24 us  [iterate(): back = lax.all_to_all(done, ('dp', 'list'), 0, 0, tiled=True)]
    pallas_call x1, Pallas kernels: 4.09 us -> 2.87 us  [finish(): call(partial(unpack_kernel, cap, owners, slices), (shape((rows, width), j...]
    unnamed x10, local copies, waits for them, and re-layouts: 2.14 us -> 3.26 us
  transfers between devices with their start and end apart: 3 -> 3, of which waited for: 2 -> 3; matrix products, arithmetic and copies ran while one was open for 1% -> 1% of each run, Pallas kernels for 20% -> 11%
where the time goes in v2:
time: 95.9 us; the launch traced here: 94.4 us
  waiting for transfers between devices  48.2 us (50%)
  Pallas kernels  20.6 us (21%)
  starting transfers between devices  20 us (21%)
  local copies, waits for them, and re-layouts  4.17 us (4%)
  between operations  1.38 us (1%)
    all_to_all x1, waiting for transfers between devices, iterate(): lax.all_to_all(packed.reshape(peers, block, LANES), ('dp', 'list'), 0, 0,...  23.5 us
    all_to_all x1, waiting for transfers between devices, iterate(): back = lax.all_to_all(done, ('dp', 'list'), 0, 0, tiled=True)  21.1 us
    all_to_all x1, starting transfers between devices, iterate(): lax.all_to_all(packed.reshape(peers, block, LANES), ('dp', 'list'), 0, 0,...  11.2 us
    pallas_call x1, Pallas kernels, iterate(): call(partial(cells_kernel, cap, peers, lists_here), shape((peers, cap, LA...  10.5 us
    all_to_all x1, starting transfers between devices, iterate(): back = lax.all_to_all(done, ('dp', 'list'), 0, 0, tiled=True)  5.24 us
    pallas_call x1, Pallas kernels, iterate(): call(partial(pack_kernel, cap, owners, slices, lists_here), (shape((slice...  4.05 us
    all_to_all x1, waiting for transfers between devices, iterate(): new_parts = lax.all_to_all(new_part, 'dp', 0, 0, tiled=True)  3.62 us
    all_to_all x1, starting transfers between devices, iterate(): new_parts = lax.all_to_all(new_part, 'dp', 0, 0, tiled=True)  3.56 us
  transfers between devices with their start and end apart: 3, of which 3 were waited for; matrix products, arithmetic and copies ran while one was open for 1% of the time, Pallas kernels for 11%

profile of v2, /device:TPU:0, one launch (start us, length us, event | category | flops | bytes accessed | tf_op | source)
XLA Modules:
  0.0 94.4 jit_solution(16553751153859171107)
XLA Ops:
  0.6 4.0 %pack.3 = (bf16[8,768,128]{2,1,0:T(8,128)(2,1)}, s32[1,512]{1,0:T(1,128)S(1)}) custom-call(s32[4,128]{1,0:T(4,128)} %bitcast.13, s32[4,128]{1,0:T(4,128)} %bitcast.15, s32[64,128]{1,0:T(8,128)} %bitcast.11, bf16[512,1024]{1,0:T(8,128)(2,1)} %rows_ref.1), custom_call_target="tpu_custom_call" | custom-call | flops 1610612736 | bytes 4194304 | tf_op jit(solution)/shard_map/pack/pallas_call | solution.py:224
  4.7 11.2 %all-to-all-start.3 = ((bf16[128,48,128]{2,1,0:T(8,128)(2,1)}), bf16[128,48,128]{2,1,0:T(8,128)(2,1)S(1)}, u32[]{:S(2)}, u32[]{:S(2)}) async-start(bf16[128,48,128]{2,1,0:T(8,128)(2,1)} %bitcast.6), calls=%async_computation.3 | async-start | bytes 3145728 | tf_op jit(solution)/shard_map/all_to_all | solution.py:234
  15.9 0.9 constant_dynamic-slice_fusion.1.old_ref
  16.8 23.5 %all-to-all-done.3.got_ref = bf16[128,48,128]{2,1,0:T(8,128)(2,1)S(1)} async-done(((bf16[128,48,128]{2,1,0:T(8,128)(2,1)}), bf16[128,48,128]{2,1,0:T(8,128)(2,1)S(1)}, u32[]{:S(2)}, u32[]{:S(2)}) %all-to-all-start.3) | async-done | bytes 1572896 | tf_op jit(solution)/shard_map/all_to_all | solution.py:234
  40.3 3.2 %lists.3 = (bf16[40,128,256]{2,1,0:T(8,128)(2,1)S(1)}, s32[128,128]{1,0:T(8,128)S(1)}, s32[16,128]{1,0:T(8,128)S(1)}, bf16[512,256]{1,0:T(8,128)(2,1)S(1)}, bf16...) custom-call(bf16[128,48,128]{2,1,0:T(8,128)(2,1)S(1)} %all-to-all-done.3.got_ref, ...), custom_call_target="tpu_custom_call" | custom-call | flops 1342177280 | bytes 4194304 | tf_op jit(solution)/shard_map/lists/pallas_call | solution.py:236
  43.6 0.0 copy-start.2
  43.6 1.5 %copy-done.2 = bf16[40,128,256]{2,1,0:T(8,128)(2,1)} copy-done((bf16[40,128,256]{2,1,0:T(8,128)(2,1)}, bf16[40,128,256]{2,1,0:T(8,128)(2,1)S(1)}, u32[]{:S(2)}) %copy-start.2) | copy-done | bytes 2621464
  45.1 3.6 %all-to-all-start.5 = ((bf16[8,512,128]{2,1,0:T(8,128)(2,1)}), bf16[8,512,128]{2,1,0:T(8,128)(2,1)S(1)}, u32[]{:S(2)}, u32[]{:S(2)}) async-start(bf16[8,512,128]{2,1,0:T(8,128)(2,1)} %get-tuple-element.51), calls=%async_computation.5 | async-start | bytes 2097152 | tf_op jit(solution)/shard_map/all_to_all | solution.py:253
  48.7 0.0 copy-start.3
  48.7 1.7 %copy-done.3 = bf16[40,128,256]{2,1,0:T(8,128)(2,1)S(1)} copy-done((bf16[40,128,256]{2,1,0:T(8,128)(2,1)S(1)}, bf16[40,128,256]{2,1,0:T(8,128)(2,1)}, u32[]{:S(2)}) %copy-start.3) | copy-done | bytes 2621464
  50.4 10.5 %cells.3 = bf16[128,40,128]{2,1,0:T(8,128)(2,1)} custom-call(bf16[40,128,256]{2,1,0:T(8,128)(2,1)S(1)} %copy-done.3, s32[128,128]{1,0:T(8,128)S(1)} %get-tuple-element.47.key_ref, s32[16,128]{1,0:T(8,128)S(1)} %get-tuple-element.48.span_ref, bf16[512,256]{1,0:T(8,128)(2,1)S(1)} %get-tuple-element.49.split_ref), custom_call_target="tpu_custom_call" | custom-call | flops 13421772800 | bytes 4194304 | tf_op jit(solution)/shard_map/cells/pallas_call | solution.py:254
  60.9 0.0 copy-start.10
  60.9 0.0 copy-start.11
  60.9 0.0 copy-start.12
  60.9 3.6 %all-to-all-done.5 = bf16[8,512,128]{2,1,0:T(8,128)(2,1)S(1)} async-done(((bf16[8,512,128]{2,1,0:T(8,128)(2,1)}), bf16[8,512,128]{2,1,0:T(8,128)(2,1)S(1)}, u32[]{:S(2)}, u32[]{:S(2)}) %all-to-all-start.5) | async-done | bytes 1048608 | tf_op jit(solution)/shard_map/all_to_all | solution.py:253
  64.5 5.2 %all-to-all-start.4 = ((bf16[128,40,128]{2,1,0:T(8,128)(2,1)}), bf16[128,40,128]{2,1,0:T(8,128)(2,1)S(1)}, u32[]{:S(2)}, u32[]{:S(2)}) async-start(bf16[128,40,128]{2,1,0:T(8,128)(2,1)} %cells.3), calls=%async_computation.4 | async-start | bytes 2621440 | tf_op jit(solution)/shard_map/all_to_all | solution.py:264
  70.5 21.1 %all-to-all-done.4 = bf16[128,40,128]{2,1,0:T(8,128)(2,1)S(1)} async-done(((bf16[128,40,128]{2,1,0:T(8,128)(2,1)}), bf16[128,40,128]{2,1,0:T(8,128)(2,1)S(1)}, u32[]{:S(2)}, u32[]{:S(2)}) %all-to-all-start.4) | async-done | bytes 1310752 | tf_op jit(solution)/shard_map/all_to_all | solution.py:264
  91.5 0.0 copy-done.10
  91.5 0.0 copy-done.11
  91.5 0.0 copy-done.12
  91.5 2.9 %conditional.1 = ((bf16[512,1024]{1,0:T(8,128)(2,1)}, f32[512,1024]{1,0:T(8,128)})) conditional(s32[]{:T(128)} %bitcast.7, (bf16[128,40,128]{2,1,0:T(8,128)(2,1)S(1)}, s32[1,512]{1,0:T(1,128)S(1)}, bf16[8,512,128]{2,1,0:T(8,128)(2,1)S(1)}) %tuple.13, (s32[4,128]{1,0:T(4,128)S(1)}, s32[4,128]{1,0:T(4,128)S(1)}, s32[64,128]{1,0:T(8,128)S(1)}, ...), branch_computations={%region_0.0_spmd, %region_1.0_spmd} | conditional | flops 85630910464 | bytes 107479408 | solution.py:298
  91.5 2.9 %unpack.2 = (bf16[512,1024]{1,0:T(8,128)(2,1)}, f32[512,1024]{1,0:T(8,128)}) custom-call(s32[1,512]{1,0:T(1,128)S(1)} %get-tuple-element.18.placed_ref, bf16[8,640,128]{2,1,0:T(8,128)(2,1)S(1)} %bitcast.10, bf16[8,512,128]{2,1,0:T(8,128)(2,1)S(1)} %get-tuple-element.20.parts_ref), custom_call_target="tpu_custom_call" | custom-call | flops 671088640 | bytes 4194304 | tf_op jit(solution)/shard_map/cond/branch_0_fun/unpack/pallas_call | solution.py:267
Async XLA Ops:
  4.7 35.6 %all-to-all-start.3 = ((bf16[128,48,128]{2,1,0:T(8,128)(2,1)}), bf16[128,48,128]{2,1,0:T(8,128)(2,1)S(1)}, u32[]{:S(2)}, u32[]{:S(2)}) async-start(bf16[128,48,128]{2,1,0:T(8,128)(2,1)} %bitcast.6), calls=%async_computation.3 | async-start | bytes 3145728 | tf_op jit(solution)/shard_map/all_to_all | solution.py:234
  43.6 1.5 %copy-start.2 = (bf16[40,128,256]{2,1,0:T(8,128)(2,1)}, bf16[40,128,256]{2,1,0:T(8,128)(2,1)S(1)}, u32[]{:S(2)}) copy-start(bf16[40,128,256]{2,1,0:T(8,128)(2,1)S(1)} %get-tuple-element.46.aug_ref) | copy-start | bytes 7864324
  45.1 19.4 %all-to-all-start.5 = ((bf16[8,512,128]{2,1,0:T(8,128)(2,1)}), bf16[8,512,128]{2,1,0:T(8,128)(2,1)S(1)}, u32[]{:S(2)}, u32[]{:S(2)}) async-start(bf16[8,512,128]{2,1,0:T(8,128)(2,1)} %get-tuple-element.51), calls=%async_computation.5 | async-start | bytes 2097152 | tf_op jit(solution)/shard_map/all_to_all | solution.py:253
  48.7 1.7 %copy-start.3 = (bf16[40,128,256]{2,1,0:T(8,128)(2,1)S(1)}, bf16[40,128,256]{2,1,0:T(8,128)(2,1)}, u32[]{:S(2)}) copy-start(bf16[40,128,256]{2,1,0:T(8,128)(2,1)} %copy-done.2) | copy-start | bytes 7864324
  60.9 30.6 %copy-start.10 = (s32[8192]{0:T(1024)S(1)}, s32[8192]{0:T(1024)}, u32[]{:S(2)}) copy-start(s32[8192]{0:T(1024)} %param.10) | copy-start | bytes 98308
  60.9 30.6 %copy-start.11 = (s32[512]{0:T(512)S(1)}, s32[512]{0:T(512)}, u32[]{:S(2)}) copy-start(s32[512]{0:T(512)} %param.8) | copy-start | bytes 6148
  60.9 30.6 %copy-start.12 = (s32[512]{0:T(512)S(1)}, s32[512]{0:T(512)}, u32[]{:S(2)}) copy-start(s32[512]{0:T(512)} %param.9) | copy-start | bytes 6148
  64.5 27.0 %all-to-all-start.4 = ((bf16[128,40,128]{2,1,0:T(8,128)(2,1)}), bf16[128,40,128]{2,1,0:T(8,128)(2,1)S(1)}, u32[]{:S(2)}, u32[]{:S(2)}) async-start(bf16[128,40,128]{2,1,0:T(8,128)(2,1)} %cells.3), calls=%async_computation.4 | async-start | bytes 2621440 | tf_op jit(solution)/shard_map/all_to_all | solution.py:264
